TPU v7x, 256 devices: a whole 4x4x8 slice. The times are simulated.
256 devices in a mesh: stem: 16 (over x, y_lo, core), grp: 16 (over z, y_hi).
Axes of the slice: x: 4, y: 4 (y_hi: 2, y_lo: 2; y = y_hi * 2 + y_lo), z: 8, core: 2. Of those that a mesh axis runs over, the one named last changes fastest.
Arguments:
- stem_tensor: float32 [256, 512, 512], P(None, 'stem', 'grp'), may hold values from -6 to 6
- left_factors: float32 [2, 16, 16, 256], P(None, 'grp'), may hold values from -0.375 to 0.375
- right_factors: float32 [2, 256, 1024], replicated, may hold values from -0.1875 to 0.1875
- index_labels: int32 [2, 9], replicated, may hold values from 0 to 8, each once within a row
Outputs:
- contracted: float32 [256, 512, 512], P(('stem', 'grp'))
Inputs may be any that keep to these rules, and one draw needn't show every extreme that they name: `index_labels`: each row is a permutation of 0 to 8.
All inputs are finite; a program needn't handle non-finite values.
Results may differ from a plain program's by a relative error of at most 0.000098.
Values sent between devices are 32-bit elements; how exact they have to be, the bound alone decides.
A program may use at most 64 MiB of HBM per device.

v0:
```python
import jax
import jax.numpy as jnp
from jax import lax
from jax.sharding import PartitionSpec as P

LOW = 32


def copy_for_each(shard, axis):
    count = lax.axis_size(axis)
    return lax.all_to_all(
        jnp.broadcast_to(shard[None], (count, *shard.shape)), axis, 0, 0, tiled=True
    )


def laid_out(tiles, dim):
    dims = list(tiles.shape[1:])
    dims[dim] *= tiles.shape[0]
    return jnp.moveaxis(tiles, 0, dim).reshape(dims)


def collect(shard, axis, dim):
    tiles = copy_for_each(shard, axis)
    return laid_out(tiles, dim)


def split_up(shard, dim, count):
    before, after = (shard.shape[:dim], shard.shape[dim + 1 :])
    return jnp.moveaxis(shard.reshape(*before, count, -1, *after), dim, 0)


def joined_exchange(shard, axis, axes, splits, concats):
    sizes = [lax.axis_size(a) for a in axes]
    tiles = split_up(shard, splits[0], sizes[0])
    tiles = jnp.moveaxis(split_up(tiles, splits[1] + 1, sizes[1]), 0, 1)
    inside = tiles.shape[2:]
    tiles = tiles.reshape(-1, *inside)
    tiles = lax.all_to_all(tiles, axis, split_axis=0, concat_axis=0, tiled=True)
    tiles = laid_out(tiles.reshape(*sizes, *inside), concats[0] + 1)
    return laid_out(tiles, concats[1])


def assemble(left, right):
    upper = left.shape[1]
    table = right.reshape(right.shape[0], LOW, LOW)
    product = jnp.einsum("abk,kcd->acbd", left, table, precision=lax.Precision.HIGHEST)
    return product.reshape(left.shape[0] * LOW, upper * LOW)


def relabel(branch, bit_order):
    row_ids = jnp.arange(branch.shape[0], dtype=jnp.int32)
    source_rows = jnp.zeros_like(row_ids)
    for bit_number in range(bit_order.shape[0]):
        picked = jnp.bitwise_and(jnp.right_shift(row_ids, bit_number), 1)
        source_rows = source_rows + jnp.left_shift(picked, bit_order[bit_number])
    return jnp.take(branch, source_rows, axis=0)


def contract_last(tensor, branch):
    dims = tensor.shape
    flat = jnp.dot(tensor.reshape(-1, dims[-1]), branch, precision=lax.Precision.HIGHEST)
    return flat.reshape(dims[:-1] + (branch.shape[1],))


def on_device(stem_tensor, left_factors, right_factors, index_labels):
    whole_left = collect(left_factors, "grp", 1)
    branches = jnp.stack(
        [assemble(whole_left[branch_id], right_factors[branch_id]) for branch_id in range(2)]
    )
    branch_one = relabel(branches[0], index_labels[0])
    branch_two = relabel(branches[1], index_labels[1])
    stem_count = lax.axis_size("stem")
    open_rows, outer_local, inner_local = stem_tensor.shape
    shaped = stem_tensor.reshape(stem_count, open_rows // stem_count, outer_local, inner_local)
    regrouped = joined_exchange(shaped, ("stem", "grp"), ("stem", "grp"), (0, 1), (2, 3))
    gathered_modes = contract_last(regrouped, branch_one)
    slab = gathered_modes[0]
    return lax.dot_general(
        slab, branch_two, (((1,), (0,)), ((), ())), precision=lax.Precision.HIGHEST
    )


def solution(mesh):
    placed = (P(None, "stem", "grp"), P(None, "grp", None, None), P(), P())
    return jax.shard_map(
        on_device,
        mesh=mesh,
        in_specs=placed,
        out_specs=P(("stem", "grp"), None, None),
        check_vma=False,
    )
```

profile of v0, /device:TPU:29, one launch (start us, length us, event | category | flops | bytes accessed | tf_op | source)
XLA Modules:
  0.0 100.2 jit_solution(14402350737959221107)
XLA Ops:
  0.0 1.6 %broadcast_in_dim.18 = f32[16,2,1,16,256]{4,3,2,1,0:T(8,128)} broadcast(f32[2,16,256]{2,1,0:T(8,128)} %bitcast.74), dimensions={1,3,4} | broadcast | bytes 557056 | tf_op jit(solution)/shard_map/broadcast_in_dim | solution.py:12
  1.6 10.9 %all-to-all-start = ((f32[16,2,1,16,256]{4,3,2,1,0:T(8,128)}), f32[16,2,1,16,256]{4,3,2,1,0:T(8,128)S(1)}, u32[]{:S(2)}, u32[]{:S(2)}) async-start(f32[16,2,1,16,256]{4,3,2,1,0:T(8,128)} %broadcast_in_dim.18), calls=%async_computation | async-start | bytes 1048576 | tf_op jit(solution)/shard_map/all_to_all | solution.py:11
  12.5 5.3 %copy.16 = f32[256,32,32]{2,1,0:T(8,128)} copy(f32[256,32,32]{0,2,1:T(8,128)} %param.6) | data formatting | bytes 2097152 | tf_op args[0]
  17.8 4.6 %reshape.86 = f32[256,1,1024]{2,1,0:T(1,128)} reshape(f32[256,1,1,32,32]{4,3,2,1,0:T(8,128)} %bitcast.67) | data formatting | bytes 2097152
  22.5 4.3 %all-to-all-done = f32[16,2,1,16,256]{4,3,2,1,0:T(8,128)S(1)} async-done(((f32[16,2,1,16,256]{4,3,2,1,0:T(8,128)}), f32[16,2,1,16,256]{4,3,2,1,0:T(8,128)S(1)}, u32[]{:S(2)}, u32[]{:S(2)}) %all-to-all-start) | async-done | bytes 524320 | tf_op jit(solution)/shard_map/all_to_all | solution.py:11
  26.8 0.0 copy-start.1
  26.8 0.8 copy-done.1
  27.6 12.4 %all-to-all-start.1 = ((f32[256,1,1024]{2,1,0:T(1,128)}), f32[256,1,1024]{2,1,0:T(1,128)}, u32[]{:S(2)}, u32[]{:S(2)}) async-start(f32[256,1,1024]{2,1,0:T(1,128)} %reshape.86), calls=%async_computation.1 | async-start | bytes 2097152 | tf_op jit(solution)/shard_map/all_to_all | solution.py:38
  40.0 0.0 copy-start.2
  40.0 1.7 %fusion.9 = (f32[1,256,1024]{2,1,0:T(8,128)S(1)}, f32[1,256,1024]{2,1,0:T(8,128)S(1)}) fusion(f32[2,256,1024]{2,1,0:T(8,128)} %param.8), kind=kLoop, calls=%fused_computation.32 | loop fusion | bytes 4194304 | tf_op jit(solution)/shard_map/slice | solution.py:68
  41.7 0.3 copy.18
  42.1 0.3 copy.13
  42.4 0.0 copy-done.2
  42.4 0.7 fusion.10
  43.1 5.6 %compare_and_fusion = (pred[512]{0:T(512)(128)(4,1)S(1)}, s32[512]{0:T(512)S(1)}) fusion(s32[]{:T(128)} %bitcast.30, s32[]{:T(128)} %bitcast.29, s32[]{:T(128)} %bitcast.28, s32[]{:T(128)} %bitcast.27, s32[]{:T(128)} %bitcast.26, s32[]{:T(128)} %bitcast.25, s32[]{:T(128)} %bitcast.24, s32[]{:T(128)} %bitcast.23, s32[]{:T(128)} %bitcast.22), kind=kLoop, calls=%fused_computation.28 | loop fusion | flops 20992 | bytes 2596 | tf_op jit(solution)/shard_map/jit(_take)/and | solution.py:56
  48.7 5.5 %compare_and_fusion.1 = (pred[512]{0:T(512)(128)(4,1)S(1)}, s32[512]{0:T(512)S(1)}) fusion(s32[]{:T(128)} %bitcast.8, s32[]{:T(128)} %bitcast.7, s32[]{:T(128)} %bitcast.6, s32[]{:T(128)} %bitcast.5, s32[]{:T(128)} %bitcast.4, s32[]{:T(128)} %bitcast.3, s32[]{:T(128)} %bitcast.2, s32[]{:T(128)} %bitcast.1, s32[]{:T(128)} %bitcast), kind=kLoop, calls=%fused_computation.29 | loop fusion | flops 20992 | bytes 2596 | tf_op jit(solution)/shard_map/jit(_take)/and | solution.py:56
  54.3 1.1 %copy.23 = f32[16,2,1,16,256]{4,3,0,2,1:T(8,128)S(1)} copy(f32[16,2,1,16,256]{4,3,2,1,0:T(8,128)} %copy-done.1) | data formatting | bytes 1048576 | tf_op jit(solution)/shard_map/all_to_all | solution.py:11
  55.4 3.4 %convolution_bitcast_fusion.1 = f32[16,32,16,32]{3,2,0,1:T(8,128)S(1)} fusion(f32[256,32,32,1]{0,2,3,1:T(8,128)S(1)} %bitcast.71, f32[2,16,1,16,256]{4,3,1,2,0:T(8,128)S(1)} %bitcast.72), kind=kOutput, calls=%fused_computation.3 | convolution fusion | flops 805306368 | bytes 2359296 | tf_op jit(solution)/shard_map/abk,kcd->acbd/dot_general | solution.py:46
  58.8 2.4 %copy.15 = f32[16,32,16,32]{3,2,1,0:T(8,128)} copy(f32[16,32,16,32]{3,2,0,1:T(8,128)S(1)} %convolution_bitcast_fusion.1) | data formatting | bytes 2097152 | tf_op jit(solution)/shard_map/abk,kcd->acbd/transpose | solution.py:46
  61.2 3.5 %squeeze_stack_reshape.6 = f32[512,512]{1,0:T(8,128)S(1)} reshape(f32[16,32,16,32]{3,2,1,0:T(8,128)} %copy.15) | data formatting | bytes 2097152 | tf_op jit(solution)/shard_map/squeeze;stack;reshape | solution.py:70
  64.8 3.4 %convolution_bitcast_fusion = f32[16,32,16,32]{3,2,0,1:T(8,128)S(1)} fusion(f32[256,32,32,1]{0,2,3,1:T(8,128)S(1)} %bitcast.70, f32[2,16,1,16,256]{4,3,1,2,0:T(8,128)S(1)} %bitcast.73), kind=kOutput, calls=%fused_computation.2 | convolution fusion | flops 805306368 | bytes 2359296 | tf_op jit(solution)/shard_map/abk,kcd->acbd/dot_general | solution.py:46
  68.2 2.4 %copy.19 = f32[16,32,16,32]{3,2,1,0:T(8,128)} copy(f32[16,32,16,32]{3,2,0,1:T(8,128)S(1)} %convolution_bitcast_fusion) | data formatting | bytes 2097152 | tf_op jit(solution)/shard_map/abk,kcd->acbd/transpose | solution.py:46
  70.6 3.5 %squeeze_stack_reshape.7 = f32[512,512]{1,0:T(8,128)S(1)} reshape(f32[16,32,16,32]{3,2,1,0:T(8,128)} %copy.19) | data formatting | bytes 2097152 | tf_op jit(solution)/shard_map/squeeze;stack;reshape | solution.py:71
  74.2 2.4 %gather_fusion = f32[512,512]{1,0:T(8,128)} fusion(f32[512,512]{1,0:T(8,128)S(1)} %squeeze_stack_reshape.6, s32[1024]{0:T(1024)S(1)} %pad_clamp_fusion.1), kind=kCustom, calls=%fused_computation.clone | custom fusion | bytes 2099200 | tf_op jit(solution)/shard_map/jit(_take)/gather | solution.py:56
  76.5 1.8 %gather_fusion.1 = f32[512,512]{1,0:T(8,128)S(1)} fusion(f32[512,512]{1,0:T(8,128)S(1)} %squeeze_stack_reshape.7, s32[1024]{0:T(1024)S(1)} %pad_clamp_fusion), kind=kCustom, calls=%fused_computation.1.clone | custom fusion | bytes 2099200 | tf_op jit(solution)/shard_map/jit(_take)/gather | solution.py:56
  78.4 0.0 all-to-all-done.1
  78.4 0.5 broadcast.86
  78.9 4.4 %reduce = f32[256,1024]{1,0:T(8,128)S(1)} reduce(f32[256,1,1024]{2,1,0:T(1,128)} %all-to-all-done.1, f32[]{:T(128)} %broadcast.86), dimensions={1}, to_apply=%all_to_all.7.reduce_sub_computation | reduce | bytes 2097156 | tf_op jit(solution)/shard_map/all_to_all | solution.py:38
  83.3 2.7 %reshape.87 = f32[256,1,1,32,32]{4,3,2,1,0:T(8,128)} reshape(f32[256,1024]{1,0:T(8,128)S(1)} %reduce) | data formatting | bytes 2097152
  86.0 5.6 %copy.17 = f32[16,1,1,16,32,32]{4,3,5,0,2,1:T(8,128)} copy(f32[16,1,1,16,32,32]{5,4,0,3,2,1:T(8,128)} %bitcast.68) | data formatting | bytes 2097152 | tf_op jit(solution)/shard_map/transpose | solution.py:19
  91.6 0.0 copy-start
  91.6 3.6 %reshape.59 = f32[16,1,1,512,32]{3,4,0,2,1:T(8,128)S(1)} reshape(f32[16,1,1,16,32,32]{4,3,5,0,2,1:T(8,128)} %copy.17) | data formatting | bytes 2097152 | tf_op jit(solution)/shard_map/reshape | solution.py:19
  95.3 0.0 copy-done
  95.3 2.0 %fusion.1 = f32[512,512]{1,0:T(8,128)S(1)} fusion(f32[512,512]{0,1:T(8,128)S(1)} %bitcast.69, f32[512,512]{1,0:T(8,128)S(1)} %copy-done, pred[512]{0:T(512)(128)(4,1)S(1)} %get-tuple-element.8), kind=kOutput, calls=%fused_computation.6 | convolution fusion | flops 1610874880 | bytes 3146240 | tf_op jit(solution)/shard_map/dot_general | solution.py:61
  97.2 3.0 %convolution_bitcast_fusion.2 = f32[1,512,512]{2,1,0:T(8,128)} fusion(f32[512,512]{1,0:T(8,128)S(1)} %fusion.1, f32[512,512]{1,0:T(8,128)S(1)} %gather_fusion.1, pred[512]{0:T(512)(128)(4,1)S(1)} %get-tuple-element.6), kind=kOutput, calls=%fused_computation.4 | convolution fusion | flops 1610874880 | bytes 3146240 | tf_op jit(solution)/shard_map/dot_general | solution.py:78
  (2 shorter events, 0.0 us)
Async XLA Ops:
  1.6 25.2 %all-to-all-start = ((f32[16,2,1,16,256]{4,3,2,1,0:T(8,128)}), f32[16,2,1,16,256]{4,3,2,1,0:T(8,128)S(1)}, u32[]{:S(2)}, u32[]{:S(2)}) async-start(f32[16,2,1,16,256]{4,3,2,1,0:T(8,128)} %broadcast_in_dim.18), calls=%async_computation | async-start | bytes 1048576 | tf_op jit(solution)/shard_map/all_to_all | solution.py:11
  26.8 0.8 copy-start.1
  27.6 50.8 %all-to-all-start.1 = ((f32[256,1,1024]{2,1,0:T(1,128)}), f32[256,1,1024]{2,1,0:T(1,128)}, u32[]{:S(2)}, u32[]{:S(2)}) async-start(f32[256,1,1024]{2,1,0:T(1,128)} %reshape.86), calls=%async_computation.1 | async-start | bytes 2097152 | tf_op jit(solution)/shard_map/all_to_all | solution.py:38
  40.0 2.4 %copy-start.2 = (s32[2,9]{1,0:T(2,128)S(1)}, s32[2,9]{1,0:T(2,128)}, u32[]{:S(2)}) copy-start(s32[2,9]{1,0:T(2,128)} %param.9) | copy-start | bytes 220
  91.6 3.6 %copy-start = (f32[512,512]{1,0:T(8,128)S(1)}, f32[512,512]{1,0:T(8,128)}, u32[]{:S(2)}) copy-start(f32[512,512]{1,0:T(8,128)} %gather_fusion) | copy-start | bytes 3145732
where the time goes:
time: 102 us; the launch traced here: 100 us
  local copies, waits for them, and re-layouts  45.1 us (44%)
  starting transfers between devices  23.3 us (23%)
  other arithmetic  15.5 us (15%)
  matrix products  11.8 us (12%)
  waiting for transfers between devices  4.31 us (4%)
    unnamed x9, local copies, waits for them, and re-layouts  13.5 us
    all_to_all x1, starting transfers between devices, joined_exchange(): tiles = lax.all_to_all(tiles, axis, split_axis=0, concat_axis=0, tiled=True)  12.4 us
    and x2, other arithmetic, relabel(): return jnp.take(branch, source_rows, axis=0)  11.1 us
    all_to_all x1, starting transfers between devices, copy_for_each(): lax.all_to_all(jnp.broadcast_to(shard[None], (count, *shard.shape)), axis...  10.9 us
    dot_general x2, matrix products, assemble(): jnp.einsum('abk,kcd->acbd', left, table, precision=lax.Precision.HIGHEST)  6.89 us
    transpose x1, local copies, waits for them, and re-layouts, laid_out(): return jnp.moveaxis(tiles, 0, dim).reshape(dims)  5.63 us
    transpose x2, local copies, waits for them, and re-layouts, assemble(): jnp.einsum('abk,kcd->acbd', left, table, precision=lax.Precision.HIGHEST)  4.78 us
    all_to_all x1, other arithmetic, joined_exchange(): tiles = lax.all_to_all(tiles, axis, split_axis=0, concat_axis=0, tiled=True)  4.36 us
  transfers between devices with their start and end apart: 2, of which 1 were waited for; matrix products, arithmetic and copies ran while one was open for 48% of the time, Pallas kernels for 0%

commit v1 on v0

v1 whole, which is shorter than its diff:
```python
import jax
import jax.numpy as jnp
from jax import lax
from jax.experimental import pallas as pl
from jax.experimental.pallas import tpu as pltpu
from jax.sharding import PartitionSpec as P

MESH = pl.DeviceIdType.MESH
F32, BF16 = jnp.float32, jnp.bfloat16
OPEN, SHARED, BOND, LOW = 256, 512, 256, 32
CHUNKS = (0, 2, 1, 3)


def place():
    stem, grp = lax.axis_index("stem"), lax.axis_index("grp")
    return stem // 4, (stem // 2) % 2, stem % 2, grp // 2, grp % 2


def device(x, y_lo, core, z, y_hi):
    return x * 4 + y_lo * 2 + core, z * 2 + y_hi


def mesh_id(stem, grp):
    return {"stem": stem, "grp": grp}


def split(value):
    high = value.astype(BF16)
    return high, (value - high.astype(F32)).astype(BF16)


def swap_groups(a):
    lane = lax.broadcasted_iota(jnp.int32, a[0].shape, 1)
    low, even = lane < 64, (lane // 32) % 2 == 0

    def far(p, q):
        t = pltpu.roll(jnp.where(low, q, p), 64, 1)
        return jnp.where(low, p, t), jnp.where(low, t, q)

    def near(p, q):
        t = jnp.where(even, q, p)
        return jnp.where(even, p, pltpu.roll(t, 32, 1)), jnp.where(even, pltpu.roll(t, 96, 1), q)

    a0, a2 = far(a[0], a[2])
    a1, a3 = far(a[1], a[3])
    return near(a0, a1) + near(a2, a3)


def row_of(labels_ref, branch, index):
    source = jnp.zeros_like(index)
    for bit in range(9):
        picked = jnp.bitwise_and(jnp.right_shift(index, bit), 1)
        source = source + jnp.left_shift(picked, labels_ref[branch, bit])
    return jnp.bitwise_and(source, LOW - 1) * 16 + jnp.right_shift(source, 5)


def dot(a, b):
    return jnp.dot(a, b, preferred_element_type=F32)


def exchange(
    stem_hbm, left_hbm, right_hbm, labels_ref, acc_ref,
    stem_v, left_v, right_v, src, dst, piece, rows_in, rows_out, left_all,
    right_hi, right_lo, whole, b0_ref, b1_ref,
    load_sem, send_sem, recv_sem, row_send, row_recv, block_send, block_recv, y_sem, x_sem,
):
    x, y_lo, core, z, y_hi = place()
    stem, grp = lax.axis_index("stem"), lax.axis_index("grp")
    me = stem * 16 + grp
    y = y_hi * 2 + y_lo

    loads = [
        pltpu.make_async_copy(stem_hbm, stem_v, load_sem.at[0]),
        pltpu.make_async_copy(left_hbm, left_v, load_sem.at[1]),
        pltpu.make_async_copy(right_hbm, right_v, load_sem.at[2]),
    ]
    for load in loads:
        load.start()

    def column(k):
        return device(x, y_lo, core ^ (k // 8), lax.rem(z + (k * 3) % 8, 8), y_hi)

    def along_y(k):
        other = lax.rem(y + k, 4)
        return device(x, other % 2, core, z, other // 2)

    def along_x(k):
        return device(lax.rem(x + k, 4), y_lo, core, z, y_hi)

    barrier = pltpu.get_barrier_semaphore()

    @pl.loop(1, 16)
    def _(k):
        s, g = column(k)
        pl.semaphore_signal(barrier, inc=1, device_id=mesh_id(s, g), device_id_type=MESH)

    for k in range(1, 4):
        for s, g in (along_y(k), along_x(k)):
            pl.semaphore_signal(barrier, inc=1, device_id=mesh_id(s, g), device_id_type=MESH)

    loads[0].wait()
    for r in range(8):
        for half in range(2):
            lanes = slice(half * 128, half * 128 + 128)
            tall = jnp.concatenate([stem_v[a * 8 + r, :, lanes] for a in range(4)], axis=0)
            src[pl.ds(half * 1024 + r, 128, stride=8), :] = tall.T

    loads[1].wait()
    for b in range(2):
        row = left_v[b, pl.ds(stem, 1), :]
        for h in range(2):
            piece[b * 2 + h : b * 2 + h + 1, :] = row[:, h * 128 : h * 128 + 128]

    def slab(ref, index, count=1):
        return ref.at[pl.ds(pl.multiple_of(index * 8, 8), 8 * count), :]

    def send(s, g, dx):
        pltpu.make_async_remote_copy(
            src_ref=slab(src, s * 16 + g), dst_ref=slab(dst, me), send_sem=send_sem, recv_sem=recv_sem.at[dx],
            device_id=mesh_id(s, g), device_id_type=MESH,
        ).start()

    pl.semaphore_wait(barrier, 21)
    for k in range(1, 4):
        s, g = along_y(k)
        pl.semaphore_signal(y_sem, inc=1, device_id=mesh_id(s, g), device_id_type=MESH)

    @pl.loop(1, 16)
    def _(k):
        s, g = column(k)
        send(s, g, 0)

    pl.semaphore_wait(y_sem, 3)
    for k in range(1, 4):
        s, g = along_x(k)
        pl.semaphore_signal(x_sem, inc=1, device_id=mesh_id(s, g), device_id_type=MESH)

    @pl.loop(1, 16)
    def _(k):
        _, g = device(x, y_lo, core, lax.rem(z + (k * 3) % 8, 8), y_hi ^ (k // 8))
        pltpu.make_async_remote_copy(
            src_ref=piece, dst_ref=rows_in.at[grp], send_sem=row_send, recv_sem=row_recv,
            device_id=mesh_id(stem, g), device_id_type=MESH,
        ).start()

    def other(k, dx):
        return device(
            lax.rem(x + dx, 4), y_lo ^ (k // 8 % 2), core ^ (k // 16 % 2), lax.rem(z + (k * 3) % 8, 8), y_hi ^ (k // 32)
        )

    @pl.loop(0, 48)
    def _(n):
        q = n // 16 + 1
        s, g = device(x, y_lo ^ (q % 2), core ^ (n // 8 % 2), lax.rem(z + (n * 3) % 8, 8), y_hi ^ (q // 2))
        send(s, g, 0)

    slab_of_me = pl.ds(pl.multiple_of(me * 8, 8), 8)
    dst[slab_of_me, :] = src[slab_of_me, :]
    rows_in[pl.ds(grp, 1)] = piece[...][None]

    pl.semaphore_wait(x_sem, 3)

    rows15 = pltpu.make_async_remote_copy(
        src_ref=rows_in.at[pl.ds(0, 15)], dst_ref=rows_in.at[pl.ds(0, 15)], send_sem=row_send, recv_sem=row_recv,
        device_id=mesh_id(stem, grp), device_id_type=MESH,
    )
    rows15.wait_recv()
    for p in range(16):
        rows_out[p * 4 : p * 4 + 4, :] = rows_in[p]

    def block(s):
        return left_all.at[pl.ds(pl.multiple_of(s * 64, 64), 64), :]

    @pl.loop(1, 16)
    def _(k):
        s, _ = device(lax.rem(x + k // 4, 4), y_lo ^ (k // 2 % 2), core ^ (k % 2), z, y_hi)
        pltpu.make_async_remote_copy(
            src_ref=rows_out, dst_ref=block(stem), send_sem=block_send, recv_sem=block_recv,
            device_id=mesh_id(s, grp), device_id_type=MESH,
        ).start()

    left_all[pl.ds(pl.multiple_of(stem * 64, 64), 64), :] = rows_out[...]

    for dx in CHUNKS[1:]:
        @pl.loop(0, 64)
        def _(k):
            s, g = other(k, dx)
            send(s, g, dx)

    loads[2].wait()
    for b in range(2):
        right_hi[b], right_lo[b] = split(right_v[b])
    blocks15 = pltpu.make_async_remote_copy(
        src_ref=left_all.at[pl.ds(0, 960), :], dst_ref=left_all.at[pl.ds(0, 960), :], send_sem=block_send, recv_sem=block_recv,
        device_id=mesh_id(stem, grp), device_id_type=MESH,
    )
    blocks15.wait_recv()
    for b in range(2):
        left = jnp.concatenate([left_all[pl.ds(b * 2 + h, 256, stride=4), :] for h in range(2)], axis=1)
        left_hi, left_lo = split(left)
        for quad in range(8):
            lanes = slice(quad * 128, quad * 128 + 128)
            r_hi, r_lo = right_hi[b, :, lanes], right_lo[b, :, lanes]
            product = dot(left_hi, r_hi) + dot(left_hi, r_lo) + dot(left_lo, r_hi)
            for u4 in range(4):
                tiles = [product[(u4 * 4 + a) * 16 : (u4 * 4 + a) * 16 + 16, :] for a in range(4)]
                for q, tile in enumerate(swap_groups(tiles)):
                    whole[(quad * 4 + q) * 16 : (quad * 4 + q) * 16 + 16, u4 * 128 : u4 * 128 + 128] = tile
        if b == 0:
            index = lax.broadcasted_iota(jnp.int32, (1, SHARED), 1)
            here = lax.broadcasted_iota(jnp.int32, (SHARED, SHARED), 0)
            one_hot = jnp.where(here == row_of(labels_ref, b, index), 1.0, 0.0).astype(BF16)
            high, low = split(whole[...].T)
            b0_ref[0] = dot(high, one_hot).astype(BF16)
            b0_ref[1] = dot(low, one_hot).astype(BF16)
        else:
            index = lax.broadcasted_iota(jnp.int32, (SHARED, 1), 0)
            here = lax.broadcasted_iota(jnp.int32, (SHARED, SHARED), 1)
            one_hot = jnp.where(here == row_of(labels_ref, b, index), 1.0, 0.0).astype(BF16)
            high, low = split(whole[...])
            b1_ref[0] = dot(one_hot, high).astype(BF16)
            b1_ref[1] = dot(one_hot, low).astype(BF16)

    def nt(a, b):
        return lax.dot_general(a, b, (((1,), (1,)), ((), ())), preferred_element_type=F32)

    for number, dx in enumerate(CHUNKS):
        from_x = lax.rem(x + 4 - dx, 4)
        count = 63 if dx == 0 else 64
        pltpu.make_async_remote_copy(
            src_ref=slab(src, 0, count), dst_ref=slab(dst, 0, count), send_sem=send_sem, recv_sem=recv_sem.at[dx],
            device_id=mesh_id(stem, grp), device_id_type=MESH,
        ).wait_recv()
        rows = []
        for s in range(4):
            quads = []
            for g4 in range(4):
                tiles = []
                for h in range(4):
                    at = pl.multiple_of((from_x * 64 + s * 16 + g4 * 4 + h) * 8, 8)
                    tiles.append(dst[pl.ds(at, 8), :])
                quads.append(jnp.concatenate(swap_groups(tiles), axis=0))
            rows.append(jnp.concatenate(quads, axis=1))
        part_hi, part_lo = split(jnp.concatenate(rows, axis=0))
        half = nt(b0_ref[0], part_hi) + nt(b0_ref[0], part_lo) + nt(b0_ref[1], part_hi)
        half_hi, half_lo = split(half)
        at = pl.ds(pl.multiple_of(from_x * 128, 128), 128)
        c_hi, c_lo = b1_ref[0, at, :], b1_ref[1, at, :]
        term = dot(half_hi, c_hi) + dot(half_hi, c_lo) + dot(half_lo, c_hi)
        if number == 0:
            acc_ref[...] = term
        else:
            acc_ref[...] += term

    pltpu.make_async_remote_copy(
        src_ref=slab(src, 0, 255), dst_ref=slab(dst, 0, 255), send_sem=send_sem, recv_sem=recv_sem.at[0],
        device_id=mesh_id(stem, grp), device_id_type=MESH,
    ).wait_send()
    rows15.wait_send()
    blocks15.wait_send()


def write_out(acc_ref, out_ref, sem):
    copy = pltpu.make_async_copy(acc_ref, out_ref.at[0], sem)
    copy.start()
    copy.wait()


def on_device(stem_tensor, left_factors, right_factors, index_labels):
    hbm = pl.BlockSpec(memory_space=pltpu.HBM)
    dma = pltpu.SemaphoreType.DMA
    acc = pl.pallas_call(
        exchange,
        out_shape=jax.ShapeDtypeStruct((SHARED, SHARED), F32),
        in_specs=[hbm, hbm, hbm, pl.BlockSpec(memory_space=pltpu.SMEM)],
        out_specs=pl.BlockSpec(memory_space=pltpu.VMEM),
        scratch_shapes=[
            pltpu.VMEM((32, 32, 256), F32),
            pltpu.VMEM((2, 16, 256), F32),
            pltpu.VMEM((2, 256, 1024), F32),
            pltpu.VMEM((2048, 128), F32),
            pltpu.VMEM((2048, 128), F32),
            pltpu.VMEM((4, 128), F32),
            pltpu.VMEM((16, 4, 128), F32),
            pltpu.VMEM((64, 128), F32),
            pltpu.VMEM((1024, 128), F32),
            pltpu.VMEM((2, 256, 1024), BF16),
            pltpu.VMEM((2, 256, 1024), BF16),
            pltpu.VMEM((SHARED, SHARED), F32),
            pltpu.VMEM((2, SHARED, SHARED), BF16),
            pltpu.VMEM((2, SHARED, SHARED), BF16),
            dma((3,)), dma, dma((4,)), dma, dma, dma, dma,
            pltpu.SemaphoreType.REGULAR, pltpu.SemaphoreType.REGULAR,
        ],
        compiler_params=pltpu.CompilerParams(collective_id=0, has_side_effects=True, vmem_limit_bytes=40 * 1024 * 1024),
        name="exchange",
    )(jnp.transpose(stem_tensor, (1, 2, 0)), left_factors.reshape(2, 16, 256), right_factors, index_labels)
    return pl.pallas_call(
        write_out,
        out_shape=jax.ShapeDtypeStruct((1, SHARED, SHARED), F32),
        in_specs=[pl.BlockSpec(memory_space=pltpu.VMEM)],
        out_specs=hbm,
        scratch_shapes=[dma],
        compiler_params=pltpu.CompilerParams(vmem_limit_bytes=8 * 1024 * 1024),
        name="write_out",
    )(acc)


def solution(mesh):
    return jax.shard_map(
        on_device,
        mesh=mesh,
        in_specs=(P(None, "stem", "grp"), P(None, "grp", None, None), P(), P()),
        out_specs=P(("stem", "grp"), None, None),
        check_vma=False,
    )
```

time: 102 us -> 54.2 us (0.53)
  the two profiles are of different devices: /device:TPU:29 before, /device:TPU:1 now
where the time goes in v1:
time: 54.2 us; the launch traced here: 54 us
  Pallas kernels  49.7 us (92%)
  local copies, waits for them, and re-layouts  4.25 us (8%)
    pallas_call x1, Pallas kernels, on_device(): pl.pallas_call(exchange, out_shape=jax.ShapeDtypeStruct((SHARED, SHARED),...  48.8 us
    unnamed x8, local copies, waits for them, and re-layouts  4.25 us

profile of v1, /device:TPU:1, one launch (start us, length us, event | category | flops | bytes accessed | tf_op | source)
XLA Modules:
  0.0 54.0 jit_solution(1860258087993087774)
XLA Ops:
  0.0 0.0 copy-start
  0.0 1.6 %copy-done = f32[2,256,1024]{2,1,0:T(8,128)S(1)} copy-done((f32[2,256,1024]{2,1,0:T(8,128)S(1)}, f32[2,256,1024]{2,1,0:T(8,128)}, u32[]{:S(2)}) %copy-start) | copy-done | bytes 2097176
  1.6 0.0 copy-start.1
  1.6 1.2 %copy-done.1 = f32[256,32,32]{0,2,1:T(8,128)S(1)} copy-done((f32[256,32,32]{0,2,1:T(8,128)S(1)}, f32[256,32,32]{0,2,1:T(8,128)}, u32[]{:S(2)}) %copy-start.1) | copy-done | bytes 1048600
  2.8 0.0 copy-start.2
  2.8 0.8 %copy-done.2 = f32[2,1,16,256]{3,2,1,0:T(8,128)S(1)} copy-done((f32[2,1,16,256]{3,2,1,0:T(8,128)S(1)}, f32[2,1,16,256]{3,2,1,0:T(8,128)}, u32[]{:S(2)}) %copy-start.2) | copy-done | bytes 32792
  3.6 0.0 copy-start.3
  3.6 0.7 %copy-done.3 = s32[2,9]{1,0:T(2,128)S(1)} copy-done((s32[2,9]{1,0:T(2,128)S(1)}, s32[2,9]{1,0:T(2,128)}, u32[]{:S(2)}) %copy-start.3) | copy-done | bytes 96
  4.3 48.8 %exchange.1.acc_ref = f32[512,512]{1,0:T(8,128)S(1)} custom-call(f32[32,32,256]{2,1,0:T(8,128)S(1)} %bitcast.2, f32[2,16,256]{2,1,0:T(8,128)S(1)} %bitcast.3, f32[2,256,1024]{2,1,0:T(8,128)S(1)} %copy-done, s32[2,9]{1,0:T(2,128)S(1)} %copy-done.3), custom_call_target="tpu_custom_call" | custom-call | tf_op jit(solution)/shard_map/exchange/pallas_call | solution.py:272
  53.0 1.0 %write_out.1 = f32[1,512,512]{2,1,0:T(8,128)} custom-call(f32[512,512]{1,0:T(8,128)S(1)} %exchange.1.acc_ref), custom_call_target="tpu_custom_call" | custom-call | tf_op jit(solution)/shard_map/write_out/pallas_call | solution.py:298
Async XLA Ops:
  0.0 1.6 %copy-start = (f32[2,256,1024]{2,1,0:T(8,128)S(1)}, f32[2,256,1024]{2,1,0:T(8,128)}, u32[]{:S(2)}) copy-start(f32[2,256,1024]{2,1,0:T(8,128)} %right_hbm.1) | copy-start | bytes 6291460
  1.6 1.2 %copy-start.1 = (f32[256,32,32]{0,2,1:T(8,128)S(1)}, f32[256,32,32]{0,2,1:T(8,128)}, u32[]{:S(2)}) copy-start(f32[256,32,32]{0,2,1:T(8,128)} %param.4) | copy-start | bytes 3145732
  2.8 0.8 %copy-start.2 = (f32[2,1,16,256]{3,2,1,0:T(8,128)S(1)}, f32[2,1,16,256]{3,2,1,0:T(8,128)}, u32[]{:S(2)}) copy-start(f32[2,1,16,256]{3,2,1,0:T(8,128)} %param.5) | copy-start | bytes 98308
  3.6 0.7 %copy-start.3 = (s32[2,9]{1,0:T(2,128)S(1)}, s32[2,9]{1,0:T(2,128)}, u32[]{:S(2)}) copy-start(s32[2,9]{1,0:T(2,128)} %labels_ref.1) | copy-start | bytes 220

commit v2 on v1

v2 whole, which is shorter than its diff:
```python
import jax
import jax.numpy as jnp
from jax import lax
from jax.experimental import pallas as pl
from jax.experimental.pallas import tpu as pltpu
from jax.sharding import PartitionSpec as P

MESH = pl.DeviceIdType.MESH
F32, BF16 = jnp.float32, jnp.bfloat16
OPEN, SHARED, BOND, LOW = 256, 512, 256, 32
CHUNKS = (0, 2, 1, 3)


def place():
    stem, grp = lax.axis_index("stem"), lax.axis_index("grp")
    return stem // 4, (stem // 2) % 2, stem % 2, grp // 2, grp % 2


def device(x, y_lo, core, z, y_hi):
    return x * 4 + y_lo * 2 + core, z * 2 + y_hi


def mesh_id(stem, grp):
    return {"stem": stem, "grp": grp}


def split(value):
    high = value.astype(BF16)
    return high, (value - high.astype(F32)).astype(BF16)


def swap_groups(a):
    lane = lax.broadcasted_iota(jnp.int32, a[0].shape, 1)
    low, even = lane < 64, (lane // 32) % 2 == 0

    def far(p, q):
        t = pltpu.roll(jnp.where(low, q, p), 64, 1)
        return jnp.where(low, p, t), jnp.where(low, t, q)

    def near(p, q):
        t = jnp.where(even, q, p)
        return jnp.where(even, p, pltpu.roll(t, 32, 1)), jnp.where(even, pltpu.roll(t, 96, 1), q)

    a0, a2 = far(a[0], a[2])
    a1, a3 = far(a[1], a[3])
    return near(a0, a1) + near(a2, a3)


def row_of(labels_ref, branch, index):
    source = jnp.zeros_like(index)
    for bit in range(9):
        picked = jnp.bitwise_and(jnp.right_shift(index, bit), 1)
        source = source + jnp.left_shift(picked, labels_ref[branch, bit])
    p = jnp.right_shift(source, 5)
    return jnp.bitwise_and(source, LOW - 1) * 16 + jnp.bitwise_and(p, 1) * 8 + jnp.right_shift(p, 1)


def dot(a, b):
    return jnp.dot(a, b, preferred_element_type=F32)


def exchange(
    stem_hbm, left_hbm, right_hbm, labels_hbm, acc_ref,
    labels_ref, stem_v, left_v, right_v, src, dst, piece, rows_in, rows_out, left_all,
    right_hi, right_lo, whole, one_hot, b0_ref, b1_ref,
    load_sem, send_sem, recv_sem, row_send, row_recv, block_send, block_recv, half_send, half_recv, y_sem, x_sem,
):
    x, y_lo, core, z, y_hi = place()
    stem, grp = lax.axis_index("stem"), lax.axis_index("grp")
    me = stem * 16 + grp
    y = y_hi * 2 + y_lo

    loads = [
        pltpu.make_async_copy(stem_hbm, stem_v, load_sem.at[0]),
        pltpu.make_async_copy(left_hbm, left_v, load_sem.at[1]),
        pltpu.make_async_copy(right_hbm, right_v, load_sem.at[2]),
        pltpu.make_async_copy(labels_hbm, labels_ref, load_sem.at[3]),
    ]
    for load in loads:
        load.start()

    def column(k):
        return device(x, y_lo, core ^ (k // 8), lax.rem(z + (k * 3) % 8, 8), y_hi)

    def along_y(k):
        other = lax.rem(y + k, 4)
        return device(x, other % 2, core, z, other // 2)

    def along_x(k):
        return device(lax.rem(x + k, 4), y_lo, core, z, y_hi)

    barrier = pltpu.get_barrier_semaphore()

    @pl.loop(1, 16)
    def _(k):
        s, g = column(k)
        pl.semaphore_signal(barrier, inc=1, device_id=mesh_id(s, g), device_id_type=MESH)

    for k in range(1, 4):
        for s, g in (along_y(k), along_x(k)):
            pl.semaphore_signal(barrier, inc=1, device_id=mesh_id(s, g), device_id_type=MESH)

    loads[0].wait()
    for r in range(8):
        for half in range(2):
            lanes = slice(half * 128, half * 128 + 128)
            tall = jnp.concatenate([stem_v[a * 8 + r, :, lanes] for a in range(4)], axis=0)
            src[pl.ds(half * 1024 + r, 128, stride=8), :] = tall.T

    loads[1].wait()
    for b in range(2):
        row = left_v[b, pl.ds(stem, 1), :]
        for h in range(2):
            piece[b * 2 + h : b * 2 + h + 1, :] = row[:, h * 128 : h * 128 + 128]

    def slab(ref, index, count=1):
        return ref.at[pl.ds(pl.multiple_of(index * 8, 8), 8 * count), :]

    def send(s, g, batch):
        pltpu.make_async_remote_copy(
            src_ref=slab(src, s * 16 + g), dst_ref=slab(dst, me), send_sem=send_sem, recv_sem=recv_sem.at[batch],
            device_id=mesh_id(s, g), device_id_type=MESH,
        ).start()

    def arrived(batch):
        count = 31 if batch == 0 else 32
        pltpu.make_async_remote_copy(
            src_ref=slab(src, 0, count), dst_ref=slab(dst, 0, count), send_sem=send_sem, recv_sem=recv_sem.at[batch],
            device_id=mesh_id(stem, grp), device_id_type=MESH,
        ).wait_recv()

    def issue(batch):
        group = batch // 2
        dx = CHUNKS[group]

        @pl.loop(batch % 2 * 32, batch % 2 * 32 + 32)
        def _(k):
            if group < 3:
                near, dz = k // 8, (k * 3) % 8
            else:
                near, far = k % 8, k // 8
                dz = jnp.where(far == 7, 0, jnp.where(far % 2 == 0, 4 - (far + 1) // 2, 4 + (far + 1) // 2))
            s, g = device(
                lax.rem(x + dx, 4), y_lo ^ (near % 2), core ^ (near // 2 % 2), lax.rem(z + dz, 8), 1 - y_hi ^ (near // 4)
            )
            send(s, g, batch)

    pl.semaphore_wait(barrier, 21)

    @pl.loop(1, 8)
    def _(k):
        s, g = device(x, y_lo, core, lax.rem(z + (k * 3) % 8, 8), y_hi)
        pltpu.make_async_remote_copy(
            src_ref=piece, dst_ref=rows_in.at[z], send_sem=row_send, recv_sem=row_recv,
            device_id=mesh_id(s, g), device_id_type=MESH,
        ).start()

    for k in (2, 1, 3):
        s, g = along_y(k)
        pl.semaphore_signal(y_sem.at[k], inc=1, device_id=mesh_id(s, g), device_id_type=MESH)

    @pl.loop(1, 16)
    def _(k):
        s, g = column(k)
        send(s, g, 0)

    def other_y(k, batch):
        to = lax.rem(y + k, 4)

        @pl.loop(0, 16)
        def _(n):
            s, g = device(x, to % 2, core ^ (n // 8), lax.rem(z + (n * 3) % 8, 8), to // 2)
            send(s, g, batch)

    pl.semaphore_wait(y_sem.at[3], 1)
    other_y(1, 0)
    pl.semaphore_wait(y_sem.at[1], 1)
    other_y(3, 1)
    pl.semaphore_wait(y_sem.at[2], 1)
    for k in (2, 1, 3):
        s, g = along_x(k)
        pl.semaphore_signal(x_sem.at[k], inc=1, device_id=mesh_id(s, g), device_id_type=MESH)
    other_y(2, 1)

    slab_of_me = pl.ds(pl.multiple_of(me * 8, 8), 8)
    dst[slab_of_me, :] = src[slab_of_me, :]
    rows_in[pl.ds(z, 1)] = piece[...][None]

    loads[2].wait()
    loads[3].wait()
    for b in range(2):
        right_hi[b], right_lo[b] = split(right_v[b])
        index = lax.broadcasted_iota(jnp.int32, (1, SHARED) if b == 0 else (SHARED, 1), 1 - b)
        here = lax.broadcasted_iota(jnp.int32, (SHARED, SHARED), b)
        one_hot[b] = jnp.where(here == row_of(labels_ref, b, index), 1.0, 0.0).astype(BF16)

    rows7 = pltpu.make_async_remote_copy(
        src_ref=rows_in.at[pl.ds(0, 7)], dst_ref=rows_in.at[pl.ds(0, 7)], send_sem=row_send, recv_sem=row_recv,
        device_id=mesh_id(stem, grp), device_id_type=MESH,
    )
    rows7.wait_recv()
    for p in range(8):
        rows_out[p * 4 : p * 4 + 4, :] = rows_in[p]
    for k in range(1, 4):
        pl.semaphore_wait(x_sem.at[k], 1)

    mine = left_all.at[pl.ds(pl.multiple_of((((core * 4 + x) * 2 + y_lo) * 2 + y_hi) * 32, 32), 32), :]

    @pl.loop(1, 16)
    def _(k):
        to = lax.rem(y + k % 4, 4)
        s, g = device(lax.rem(x + k // 4, 4), to % 2, core, z, to // 2)
        pltpu.make_async_remote_copy(
            src_ref=rows_out, dst_ref=mine, send_sem=block_send, recv_sem=block_recv,
            device_id=mesh_id(s, g), device_id_type=MESH,
        ).start()

    left_all[pl.ds(pl.multiple_of((((core * 4 + x) * 2 + y_lo) * 2 + y_hi) * 32, 32), 32), :] = rows_out[...]

    issue(2)
    issue(3)
    issue(4)
    issue(5)
    issue(6)
    issue(7)
    blocks15 = pltpu.make_async_remote_copy(
        src_ref=left_all.at[pl.ds(0, 480), :], dst_ref=left_all.at[pl.ds(0, 480), :], send_sem=block_send, recv_sem=block_recv,
        device_id=mesh_id(stem, grp), device_id_type=MESH,
    )
    blocks15.wait_recv()
    half_all = left_all.at[pl.ds(pl.multiple_of(core * 512, 512), 512), :]
    s, g = device(x, y_lo, 1 - core, z, y_hi)
    half_copy = pltpu.make_async_remote_copy(
        src_ref=half_all, dst_ref=half_all, send_sem=half_send, recv_sem=half_recv,
        device_id=mesh_id(s, g), device_id_type=MESH,
    )
    half_copy.start()
    half_copy.wait_recv()

    def assemble(b):
        left = jnp.concatenate([left_all[pl.ds(b * 2 + h, 256, stride=4), :] for h in range(2)], axis=1)
        left_hi, left_lo = split(left)
        for quad in range(8):
            lanes = slice(quad * 128, quad * 128 + 128)
            r_hi, r_lo = right_hi[b, :, lanes], right_lo[b, :, lanes]
            product = dot(left_hi, r_hi) + dot(left_hi, r_lo) + dot(left_lo, r_hi)
            for u4 in range(4):
                starts = [((a % 2) * 8 + u4 * 2 + a // 2) * 16 for a in range(4)]
                for q, tile in enumerate(swap_groups([product[at : at + 16, :] for at in starts])):
                    whole[(quad * 4 + q) * 16 : (quad * 4 + q) * 16 + 16, u4 * 128 : u4 * 128 + 128] = tile
        if b == 0:
            for part, value in enumerate(split(whole[...].T)):
                b0_ref[part] = dot(value, one_hot[b]).astype(BF16)
        else:
            for part, value in enumerate(split(whole[...])):
                b1_ref[part] = dot(one_hot[b], value).astype(BF16)

    def nt(a, b):
        return lax.dot_general(a, b, (((1,), (1,)), ((), ())), preferred_element_type=F32)

    def contract(number):
        from_x = lax.rem(x + 4 - CHUNKS[number], 4)
        rows = []
        for s in range(4):
            quads = []
            for g4 in range(4):
                tiles = []
                for h in range(4):
                    at = pl.multiple_of((from_x * 64 + s * 16 + g4 * 4 + h) * 8, 8)
                    tiles.append(dst[pl.ds(at, 8), :])
                quads.append(jnp.concatenate(swap_groups(tiles), axis=0))
            rows.append(jnp.concatenate(quads, axis=1))
        part_hi, part_lo = split(jnp.concatenate(rows, axis=0))
        half = nt(b0_ref[0], part_hi) + nt(b0_ref[0], part_lo) + nt(b0_ref[1], part_hi)
        half_hi, half_lo = split(half)
        at = pl.ds(pl.multiple_of(from_x * 128, 128), 128)
        c_hi, c_lo = b1_ref[0, at, :], b1_ref[1, at, :]
        term = dot(half_hi, c_hi) + dot(half_hi, c_lo) + dot(half_lo, c_hi)
        if number == 0:
            acc_ref[...] = term
        else:
            acc_ref[...] += term

    assemble(0)
    assemble(1)
    arrived(0)
    arrived(1)
    contract(0)
    arrived(2)
    arrived(3)
    contract(1)
    arrived(4)
    arrived(5)
    contract(2)
    arrived(6)
    arrived(7)
    contract(3)

    pltpu.make_async_remote_copy(
        src_ref=slab(src, 0, 255), dst_ref=slab(dst, 0, 255), send_sem=send_sem, recv_sem=recv_sem.at[0],
        device_id=mesh_id(stem, grp), device_id_type=MESH,
    ).wait_send()
    rows7.wait_send()
    blocks15.wait_send()
    half_copy.wait_send()


def write_out(acc_ref, out_ref, sem):
    copy = pltpu.make_async_copy(acc_ref, out_ref.at[0], sem)
    copy.start()
    copy.wait()


def on_device(stem_tensor, left_factors, right_factors, index_labels):
    hbm = pl.BlockSpec(memory_space=pltpu.HBM)
    dma = pltpu.SemaphoreType.DMA
    operands = jnp.transpose(stem_tensor, (1, 2, 0)), left_factors.reshape(2, 16, 256), right_factors, index_labels
    acc = pl.pallas_call(
        exchange,
        out_shape=jax.ShapeDtypeStruct((SHARED, SHARED), F32),
        in_specs=[hbm, hbm, hbm, hbm],
        out_specs=pl.BlockSpec(memory_space=pltpu.VMEM),
        scratch_shapes=[
            pltpu.SMEM((2, 9), jnp.int32),
            pltpu.VMEM((32, 32, 256), F32),
            pltpu.VMEM((2, 16, 256), F32),
            pltpu.VMEM((2, 256, 1024), F32),
            pltpu.VMEM((2048, 128), F32),
            pltpu.VMEM((2048, 128), F32),
            pltpu.VMEM((4, 128), F32),
            pltpu.VMEM((8, 4, 128), F32),
            pltpu.VMEM((32, 128), F32),
            pltpu.VMEM((1024, 128), F32),
            pltpu.VMEM((2, 256, 1024), BF16),
            pltpu.VMEM((2, 256, 1024), BF16),
            pltpu.VMEM((SHARED, SHARED), F32),
            pltpu.VMEM((2, SHARED, SHARED), BF16),
            pltpu.VMEM((2, SHARED, SHARED), BF16),
            pltpu.VMEM((2, SHARED, SHARED), BF16),
            dma((4,)), dma, dma((8,)), dma, dma, dma, dma, dma, dma,
            pltpu.SemaphoreType.REGULAR((4,)), pltpu.SemaphoreType.REGULAR((4,)),
        ],
        compiler_params=pltpu.CompilerParams(collective_id=0, has_side_effects=True, vmem_limit_bytes=40 * 1024 * 1024),
        name="exchange",
    )(*(pltpu.with_memory_space_constraint(a, pltpu.HBM) for a in operands))
    return pl.pallas_call(
        write_out,
        out_shape=jax.ShapeDtypeStruct((1, SHARED, SHARED), F32),
        in_specs=[pl.BlockSpec(memory_space=pltpu.VMEM)],
        out_specs=hbm,
        scratch_shapes=[dma],
        compiler_params=pltpu.CompilerParams(vmem_limit_bytes=8 * 1024 * 1024),
        name="write_out",
    )(acc)


def solution(mesh):
    return jax.shard_map(
        on_device,
        mesh=mesh,
        in_specs=(P(None, "stem", "grp"), P(None, "grp", None, None), P(), P()),
        out_specs=P(("stem", "grp"), None, None),
        check_vma=False,
    )
```

time: 54.2 us -> 41.2 us (0.76)
  the two profiles are of different devices: /device:TPU:1 before, /device:TPU:29 now
where the time goes in v2:
time: 41.2 us; the launch traced here: 41.1 us
  Pallas kernels  41.1 us (100%)
    pallas_call x1, Pallas kernels, on_device(): pl.pallas_call(exchange, out_shape=jax.ShapeDtypeStruct((SHARED, SHARED),...  40.1 us
    pallas_call x1, Pallas kernels, on_device(): pl.pallas_call(write_out, out_shape=jax.ShapeDtypeStruct((1, SHARED, SHAR...  0.98 us

profile of v2, /device:TPU:29, one launch (start us, length us, event | category | flops | bytes accessed | tf_op | source)
XLA Modules:
  0.0 41.1 jit_solution(1853859031587967723)
XLA Ops:
  0.0 40.1 %exchange.1.acc_ref = f32[512,512]{1,0:T(8,128)S(1)} custom-call(f32[32,32,256]{2,1,0:T(8,128)} %bitcast.2, f32[2,16,256]{2,1,0:T(8,128)} %bitcast.3, f32[2,256,1024]{2,1,0:T(8,128)} %right_hbm.1, s32[2,9]{1,0:T(2,128)} %labels_hbm.1), custom_call_target="tpu_custom_call" | custom-call | tf_op jit(solution)/shard_map/exchange/pallas_call | solution.py:318
  40.1 1.0 %write_out.1 = f32[1,512,512]{2,1,0:T(8,128)} custom-call(f32[512,512]{1,0:T(8,128)S(1)} %exchange.1.acc_ref), custom_call_target="tpu_custom_call" | custom-call | tf_op jit(solution)/shard_map/write_out/pallas_call | solution.py:346

commit v3 on v2

--- a/solution.py
+++ b/solution.py
@@ -135,11 +135,7 @@
 
         @pl.loop(batch % 2 * 32, batch % 2 * 32 + 32)
         def _(k):
-            if group < 3:
-                near, dz = k // 8, (k * 3) % 8
-            else:
-                near, far = k % 8, k // 8
-                dz = jnp.where(far == 7, 0, jnp.where(far % 2 == 0, 4 - (far + 1) // 2, 4 + (far + 1) // 2))
+            near, dz = k // 8, (k * 3) % 8
             s, g = device(
                 lax.rem(x + dx, 4), y_lo ^ (near % 2), core ^ (near // 2 % 2), lax.rem(z + dz, 8), 1 - y_hi ^ (near // 4)
             )
@@ -240,10 +236,11 @@
     def assemble(b):
         left = jnp.concatenate([left_all[pl.ds(b * 2 + h, 256, stride=4), :] for h in range(2)], axis=1)
         left_hi, left_lo = split(left)
+        left_all_parts = jnp.concatenate([left_hi, left_hi, left_lo], axis=1)
         for quad in range(8):
             lanes = slice(quad * 128, quad * 128 + 128)
             r_hi, r_lo = right_hi[b, :, lanes], right_lo[b, :, lanes]
-            product = dot(left_hi, r_hi) + dot(left_hi, r_lo) + dot(left_lo, r_hi)
+            product = dot(left_all_parts, jnp.concatenate([r_hi, r_lo, r_hi], axis=0))
             for u4 in range(4):
                 starts = [((a % 2) * 8 + u4 * 2 + a // 2) * 16 for a in range(4)]
                 for q, tile in enumerate(swap_groups([product[at : at + 16, :] for at in starts])):
@@ -271,11 +268,17 @@
                 quads.append(jnp.concatenate(swap_groups(tiles), axis=0))
             rows.append(jnp.concatenate(quads, axis=1))
         part_hi, part_lo = split(jnp.concatenate(rows, axis=0))
-        half = nt(b0_ref[0], part_hi) + nt(b0_ref[0], part_lo) + nt(b0_ref[1], part_hi)
+        half = nt(
+            jnp.concatenate([b0_ref[0], b0_ref[0], b0_ref[1]], axis=1),
+            jnp.concatenate([part_hi, part_lo, part_hi], axis=1),
+        )
         half_hi, half_lo = split(half)
         at = pl.ds(pl.multiple_of(from_x * 128, 128), 128)
         c_hi, c_lo = b1_ref[0, at, :], b1_ref[1, at, :]
-        term = dot(half_hi, c_hi) + dot(half_hi, c_lo) + dot(half_lo, c_hi)
+        term = dot(
+            jnp.concatenate([half_hi, half_hi, half_lo], axis=1),
+            jnp.concatenate([c_hi, c_lo, c_hi], axis=0),
+        )
         if number == 0:
             acc_ref[...] = term
         else:

time: 41.2 us -> 40.6 us (0.985)
  Pallas kernels: 41.1 us -> 40.5 us
    pallas_call x1, Pallas kernels: 40.1 us -> 39.5 us  [on_device(): pl.pallas_call(exchange, out_shape=jax.ShapeDtypeStruct((SHARED, SHARED),...]
where the time goes in v3:
time: 40.6 us; the launch traced here: 40.5 us
  Pallas kernels  40.5 us (100%)
    pallas_call x1, Pallas kernels, on_device(): pl.pallas_call(exchange, out_shape=jax.ShapeDtypeStruct((SHARED, SHARED),...  39.5 us
    pallas_call x1, Pallas kernels, on_device(): pl.pallas_call(write_out, out_shape=jax.ShapeDtypeStruct((1, SHARED, SHAR...  0.98 us

profile of v3, /device:TPU:29, one launch (start us, length us, event | category | flops | bytes accessed | tf_op | source)
XLA Modules:
  0.0 40.5 jit_solution(8315639455236189138)
XLA Ops:
  0.0 39.5 %exchange.1.acc_ref = f32[512,512]{1,0:T(8,128)S(1)} custom-call(f32[32,32,256]{2,1,0:T(8,128)} %bitcast.2, f32[2,16,256]{2,1,0:T(8,128)} %bitcast.3, f32[2,256,1024]{2,1,0:T(8,128)} %right_hbm.1, s32[2,9]{1,0:T(2,128)} %labels_hbm.1), custom_call_target="tpu_custom_call" | custom-call | tf_op jit(solution)/shard_map/exchange/pallas_call | solution.py:321
  39.5 1.0 %write_out.1 = f32[1,512,512]{2,1,0:T(8,128)} custom-call(f32[512,512]{1,0:T(8,128)S(1)} %exchange.1.acc_ref), custom_call_target="tpu_custom_call" | custom-call | tf_op jit(solution)/shard_map/write_out/pallas_call | solution.py:349

commit v4 on v3

--- a/solution.py
+++ b/solution.py
@@ -182,14 +182,6 @@
     dst[slab_of_me, :] = src[slab_of_me, :]
     rows_in[pl.ds(z, 1)] = piece[...][None]
 
-    loads[2].wait()
-    loads[3].wait()
-    for b in range(2):
-        right_hi[b], right_lo[b] = split(right_v[b])
-        index = lax.broadcasted_iota(jnp.int32, (1, SHARED) if b == 0 else (SHARED, 1), 1 - b)
-        here = lax.broadcasted_iota(jnp.int32, (SHARED, SHARED), b)
-        one_hot[b] = jnp.where(here == row_of(labels_ref, b, index), 1.0, 0.0).astype(BF16)
-
     rows7 = pltpu.make_async_remote_copy(
         src_ref=rows_in.at[pl.ds(0, 7)], dst_ref=rows_in.at[pl.ds(0, 7)], send_sem=row_send, recv_sem=row_recv,
         device_id=mesh_id(stem, grp), device_id_type=MESH,
@@ -219,6 +211,14 @@
     issue(5)
     issue(6)
     issue(7)
+    loads[2].wait()
+    loads[3].wait()
+    for b in range(2):
+        right_hi[b], right_lo[b] = split(right_v[b])
+        index = lax.broadcasted_iota(jnp.int32, (1, SHARED) if b == 0 else (SHARED, 1), 1 - b)
+        here = lax.broadcasted_iota(jnp.int32, (SHARED, SHARED), b)
+        one_hot[b] = jnp.where(here == row_of(labels_ref, b, index), 1.0, 0.0).astype(BF16)
+
     blocks15 = pltpu.make_async_remote_copy(
         src_ref=left_all.at[pl.ds(0, 480), :], dst_ref=left_all.at[pl.ds(0, 480), :], send_sem=block_send, recv_sem=block_recv,
         device_id=mesh_id(stem, grp), device_id_type=MESH,

time: 40.6 us -> 40.6 us (level)
  no operation moved by 1% of the time
where the time goes in v4:
time: 40.6 us
  Pallas kernels  40.6 us (100%)
    pallas_call x1, Pallas kernels, on_device(): pl.pallas_call(exchange, out_shape=jax.ShapeDtypeStruct((SHARED, SHARED),...  39.6 us
    pallas_call x1, Pallas kernels, on_device(): pl.pallas_call(write_out, out_shape=jax.ShapeDtypeStruct((1, SHARED, SHAR...  0.98 us

profile of v4, /device:TPU:29, one launch (start us, length us, event | category | flops | bytes accessed | tf_op | source)
XLA Modules:
  0.0 40.6 jit_solution(2704403673843281172)
XLA Ops:
  0.0 39.6 %exchange.1.acc_ref = f32[512,512]{1,0:T(8,128)S(1)} custom-call(f32[32,32,256]{2,1,0:T(8,128)} %bitcast.2, f32[2,16,256]{2,1,0:T(8,128)} %bitcast.3, f32[2,256,1024]{2,1,0:T(8,128)} %right_hbm.1, s32[2,9]{1,0:T(2,128)} %labels_hbm.1), custom_call_target="tpu_custom_call" | custom-call | tf_op jit(solution)/shard_map/exchange/pallas_call | solution.py:321
  39.6 1.0 %write_out.1 = f32[1,512,512]{2,1,0:T(8,128)} custom-call(f32[512,512]{1,0:T(8,128)S(1)} %exchange.1.acc_ref), custom_call_target="tpu_custom_call" | custom-call | tf_op jit(solution)/shard_map/write_out/pallas_call | solution.py:349
